TPU v7x, 128 devices: a whole 4x4x4 slice. The times are simulated.
128 devices in a mesh: tok: 8 (over y, z_lo), hid: 16 (over z_hi, x, core).
Axes of the slice: x: 4, y: 4, z: 4 (z_hi: 2, z_lo: 2; z = z_hi * 2 + z_lo), core: 2. Of those that a mesh axis runs over, the one named last changes fastest.
Arguments:
- tokens: bfloat16 [12288, 6144], P('tok', 'hid'), may hold values from -6 to 6
- cotangent: bfloat16 [12288, 6144], P('tok', 'hid'), may hold values from -6 to 6
- expert_choice: int32 [12288, 2], P('tok'), may hold values from 0 to 7, as said below
- router: bfloat16 [8, 6144], replicated, may hold values from -0.078125 to 0.078125
- gate_up: bfloat16 [6144, 2, 8192], P('tok', None, 'hid'), may hold values from -0.109375 to 0.109375
- w_down: bfloat16 [6144, 8192], P('tok', 'hid'), may hold values from -0.0625 to 0.0625
Outputs:
- grad_tokens: bfloat16 [12288, 6144], P('tok', 'hid')
- d_combine: float32 [12288, 2], P('tok')
- d_gate_up: float32 [6144, 2, 8192], P('tok', None, 'hid')
- d_down: float32 [6144, 8192], P('tok', 'hid')
Inputs may be any that keep to these rules, and one draw needn't show every extreme that they name: `expert_choice`: each row names 2 different experts. In every aligned block of 1536 rows at most 432 rows name expert 0 and at least half of 432 do; some block has exactly 432.
All inputs are finite; a program needn't handle non-finite values.
Results may differ from a plain program's by a relative error of at most 0.017.
Values may be sent and summed in bfloat16 or wider, within the bound.
A program may use at most 128 MiB of HBM per device.

v0:
```python
import jax
import jax.numpy as jnp
from jax import lax
from jax.sharding import Mesh
from jax.sharding import PartitionSpec as P

CAP = 432
TOK = ("y", "zl")
ALL = ("y", "zl", "hid")


def swap_pairs():
    pairs = []
    for y in range(4):
        for zl in range(2):
            for h in range(16):
                to_y, to_h = (h // 4, y * 4 + h % 4)
                pairs.append(((y * 2 + zl) * 16 + h, (to_y * 2 + zl) * 16 + to_h))
    return pairs


def silu_pair(pre):
    sigma = jax.nn.sigmoid(pre)
    return (pre * sigma, sigma * (1.0 + pre * (1.0 - sigma)))


def dot_f32(left, right, dims):
    return lax.dot_general(
        left, right, ((dims[0], dims[1]), ((), ())), preferred_element_type=jnp.float32
    )


def local(tokens, cotangent, expert_choice, router, gate_up, w_down):
    cols = tokens.shape[1]
    rows_own, hid = w_down.shape
    zl = lax.axis_index("zl")
    first = expert_choice[:, 0]
    second = expert_choice[:, 1]
    in_first = first == 0
    in_second = second == 0
    routed = jnp.logical_or(in_first, in_second)
    flags = routed.astype(jnp.int32)
    slot_rank = jnp.cumsum(flags) - flags
    slot_ids = jnp.arange(CAP, dtype=jnp.int32)
    placed = jnp.logical_and(routed[None, :], slot_rank[None, :] == slot_ids[:, None])
    select = placed.astype(jnp.bfloat16)
    weights = jnp.concatenate([gate_up.reshape(rows_own, 2 * hid), w_down], axis=1)
    other_weights = lax.ppermute(weights, "zl", [(0, 1), (1, 0)])
    dispatched = dot_f32(select, jnp.concatenate([tokens, cotangent], axis=1), ((1,), (0,)))
    moved = lax.ppermute(dispatched.astype(jnp.bfloat16), ALL, swap_pairs())
    gathered = lax.all_gather(moved, "hid", axis=0)
    router_cols = lax.dynamic_slice_in_dim(router, lax.axis_index("hid") * cols, cols, 1)
    logits = dot_f32(tokens, router_cols, ((1,), (1,)))
    other = first + second
    labels = jnp.arange(logits.shape[1], dtype=jnp.int32)
    other_logit = jnp.sum(jnp.where(other[:, None] == labels[None, :], logits, 0.0), axis=1)
    margin_part = jnp.sum(jnp.where(placed, (logits[:, 0] - other_logit)[None, :], 0.0), axis=1)
    margin = lax.psum(margin_part, "hid")
    filled = jnp.any(placed, axis=1)
    slot_gate = jnp.where(filled, jax.nn.sigmoid(margin), 0.0)
    parts = gathered.reshape(4, 4, CAP, 2, cols).transpose(3, 0, 2, 1, 4)
    parts = parts.reshape(2, 4 * CAP, 4 * cols)
    rows_in, rows_cot = (parts[0], parts[1])
    low = jnp.where(zl == 0, weights, other_weights)
    high = jnp.where(zl == 0, other_weights, weights)
    both = jnp.concatenate([low, high], axis=0)
    w_gu = both[:, : 2 * hid]
    w_d = both[:, 2 * hid :]
    pre = jnp.concatenate(
        [
            dot_f32(rows_in, w_gu, ((1,), (0,))).astype(jnp.bfloat16),
            dot_f32(rows_cot, w_d, ((1,), (0,))).astype(jnp.bfloat16),
        ],
        axis=1,
    )
    pre = lax.psum_scatter(pre, "y", scatter_dimension=0, tiled=True).astype(jnp.float32)
    gate_pre, up_pre, raw = (pre[:, :hid], pre[:, hid : 2 * hid], pre[:, 2 * hid :])
    active, slope = silu_pair(gate_pre)
    product = active * up_pre
    scale = slot_gate[:, None]
    score_part = jnp.sum(product * raw, axis=1)
    upstream = scale * raw
    mids = jnp.concatenate(
        [
            (upstream * up_pre * slope).astype(jnp.bfloat16),
            (upstream * active).astype(jnp.bfloat16),
            (scale * product).astype(jnp.bfloat16),
        ],
        axis=1,
    )
    mids = lax.all_gather(mids, "y", axis=0, tiled=True)
    mid_gu, mid_d = (mids[:, : 2 * hid], mids[:, 2 * hid :])
    scores = lax.psum(score_part, "hid")
    back = dot_f32(mid_gu, w_gu, ((1,), (1,))).astype(jnp.bfloat16)
    back = back.reshape(4, CAP, 4, cols).transpose(0, 2, 1, 3).reshape(16, CAP, cols)
    back = lax.psum_scatter(back, "hid", scatter_dimension=0, tiled=False)

    def grads_of(rows):
        return jnp.concatenate(
            [
                dot_f32(lax.dynamic_slice_in_dim(rows_in, rows, rows_own, 1), mid_gu, ((0,), (0,))),
                dot_f32(lax.dynamic_slice_in_dim(rows_cot, rows, rows_own, 1), mid_d, ((0,), (0,))),
            ],
            axis=1,
        )

    sent = grads_of((1 - zl) * rows_own).astype(jnp.bfloat16)
    arrived = lax.ppermute(sent, "zl", [(0, 1), (1, 0)])
    grads = grads_of(zl * rows_own) + arrived.astype(jnp.float32)
    back = lax.ppermute(back, ALL, swap_pairs())
    grad_tokens = dot_f32(select, back, ((0,), (0,))).astype(jnp.bfloat16)
    token_score = jnp.sum(jnp.where(placed, scores[:, None], 0.0), axis=0)
    d_combine = jnp.stack(
        [jnp.where(in_first, token_score, 0.0), jnp.where(in_second, token_score, 0.0)], axis=1
    )
    d_gate_up = grads[:, : 2 * hid].reshape(rows_own, 2, hid)
    d_down = grads[:, 2 * hid :]
    return (grad_tokens, d_combine, d_gate_up, d_down)


def solution(mesh):
    split = Mesh(mesh.devices.reshape(4, 2, mesh.shape["hid"]), ("y", "zl", "hid"))
    return jax.shard_map(
        local,
        mesh=split,
        in_specs=(
            P(TOK, "hid"),
            P(TOK, "hid"),
            P(TOK, None),
            P(),
            P(TOK, None, "hid"),
            P(TOK, "hid"),
        ),
        out_specs=(P(TOK, "hid"), P(TOK, None), P(TOK, None, "hid"), P(TOK, "hid")),
        check_vma=False,
    )
```

profile of v0, /device:TPU:24, one launch (start us, length us, event | category | flops | bytes accessed | tf_op | source)
XLA Modules:
  0.0 526.6 jit_solution(5789460973194179525)
XLA Ops:
  7.2 0.8 convert_reduce_fusion
  8.7 3.1 fusion.33
  11.8 7.9 %collective-permute-start = (bf16[432,768]{1,0:T(8,128)(2,1)S(1)}, bf16[432,768]{1,0:T(8,128)(2,1)S(1)}, u32[]{:S(2)}, u32[]{:S(2)}) collective-permute-start(bf16[432,768]{1,0:T(8,128)(2,1)S(1)} %fusion.33), channel_id=1, source_target_pairs={{0,0},{1,1},{2,2},{3,3},{4,32},{5,33},{6,34},{7,35},{8,64},{9,65},... | collective-permute-start | bytes 1990664 | tf_op jit(solution)/shard_map/ppermute | solution.py:50
  19.7 16.6 %collective-permute-done = bf16[432,768]{1,0:T(8,128)(2,1)S(1)} collective-permute-done((bf16[432,768]{1,0:T(8,128)(2,1)S(1)}, bf16[432,768]{1,0:T(8,128)(2,1)S(1)}, u32[]{:S(2)}, u32[]{:S(2)}) %collective-permute-start) | collective-permute-done | bytes 663584 | tf_op jit(solution)/shard_map/ppermute | solution.py:50
  36.3 0.8 copy-done.10
  37.8 0.6 copy-done.9
  38.5 2.2 collective-permute-start.1
  40.6 76.6 %collective-permute-done.1 = bf16[768,1536]{1,0:T(8,128)(2,1)} collective-permute-done((bf16[768,1536]{1,0:T(8,128)(2,1)S(1)}, bf16[768,1536]{1,0:T(8,128)(2,1)}, u32[]{:S(2)}, u32[]{:S(2)}) %collective-permute-start.1) | collective-permute-done | bytes 2359328 | tf_op jit(solution)/shard_map/ppermute | solution.py:48
  117.3 4.2 broadcast_select_fusion.1
  121.5 18.0 %all-gather.6.cloned.1.call-done = bf16[6912,768]{1,0:T(8,128)(2,1)} async-done(((bf16[432,768]{1,0:T(8,128)(2,1)}), bf16[6912,768]{1,0:T(8,128)(2,1)}) %all-gather.6.cloned.1.call-update) | async-done | bytes 10616848 | tf_op jit(solution)/shard_map/all_gather | solution.py:51
  139.5 20.7 %reshape.96 = bf16[4,4,432,2,384]{4,3,2,1,0:T(2,128)(2,1)} reshape(bf16[6912,768]{1,0:T(8,128)(2,1)} %all-gather.6.cloned.1.call-done) | data formatting | bytes 21233664 | tf_op jit(solution)/shard_map/reshape | solution.py:61
  160.1 8.5 %copy.26 = bf16[4,4,432,2,384]{4,1,2,0,3:T(4,128)(2,1)S(1)} copy(bf16[4,4,432,2,384]{4,3,2,1,0:T(2,128)(2,1)} %reshape.96) | data formatting | bytes 21233664 | tf_op jit(solution)/shard_map/reshape | solution.py:61
  168.7 3.8 fusion.53
  172.5 1.0 copy.22
  173.5 1.0 copy.24
  174.5 1.7 copy-done.2
  176.2 0.7 copy-done.4
  176.9 2.4 copy-done.6
  179.3 6.1 %convolution_convert_fusion.1 = bf16[1728,1024]{1,0:T(8,128)(2,1)S(1)} fusion(bf16[1728,1536]{1,0:T(8,128)(2,1)S(1)} %bitcast.29, bf16[768,1536]{1,0:T(8,128)(2,1)S(1)} %copy-done.4, bf16[768,1536]{1,0:T(8,128)(2,1)S(1)} %copy-done.6), kind=kOutput, calls=%fused_computation.6 | convolution fusion | flops 5443878912 | bytes 13565952 | tf_op jit(solution)/shard_map/dot_general | solution.py:28
  185.4 3.1 convolution_convert_fusion.2
  188.5 2.8 pad_maximum_fusion
  191.4 1.2 copy-done.8
  193.0 0.4 fusion.16
  193.5 52.6 %reduce-scatter.3.cloned.1.call-done = bf16[432,1536]{1,0:T(8,128)(2,1)} async-done(((bf16[1728,1536]{1,0:T(8,128)(2,1)}), bf16[432,1536]{1,0:T(8,128)(2,1)}) %reduce-scatter.3.cloned.1.call-update) | async-done | bytes 1327120 | tf_op jit(solution)/shard_map/reduce_scatter | solution.py:76
  246.1 1.6 convert_element_type.51
  248.1 37.8 %psum.15 = f32[432]{0:T(512)S(1)} all-reduce(f32[432]{0:T(512)S(1)} %multiply_reduce_fusion), channel_id=1, replica_groups=mesh['y'=4,'zl'=2,'hid'=16] {'hid'}, use_global_device_ids=true, to_apply=%region_9.10 | all-reduce | flops 432 | bytes 3456 | tf_op jit(solution)/shard_map/psum | solution.py:93
  285.9 1.0 select_reduce_fusion
  286.9 33.4 %psum.14 = f32[432]{0:T(512)S(1)} all-reduce(f32[432]{0:T(512)S(1)} %get-tuple-element.5), channel_id=1, replica_groups=mesh['y'=4,'zl'=2,'hid'=16] {'hid'}, use_global_device_ids=true, to_apply=%region_5.6 | all-reduce | flops 432 | bytes 3456 | tf_op jit(solution)/shard_map/psum | solution.py:58
  320.3 0.6 multiply_convert_fusion.2
  320.9 1.1 pad_maximum_fusion.4
  322.1 53.0 %all-gather.4.cloned.1.call-done = bf16[1728,1536]{1,0:T(8,128)(2,1)} async-done(((bf16[432,1536]{1,0:T(8,128)(2,1)}), bf16[1728,1536]{1,0:T(8,128)(2,1)}) %all-gather.4.cloned.1.call-update) | async-done | bytes 5308432 | tf_op jit(solution)/shard_map/all_gather | solution.py:91
  375.1 9.7 %convolution_convert_fusion = bf16[1728,1536]{1,0:T(8,128)(2,1)} fusion(bf16[1728,1536]{1,0:T(8,128)(2,1)} %all-gather.4.cloned.1.call-done, bf16[768,1536]{1,0:T(8,128)(2,1)S(1)} %copy-done.5, bf16[768,1536]{1,0:T(8,128)(2,1)} %get-tuple-element.11), kind=kOutput, calls=%fused_computation.1 | convolution fusion | flops 5444763648 | bytes 13565952 | tf_op jit(solution)/shard_map/dot_general | solution.py:28
  384.9 9.7 %reshape.98 = bf16[4,432,4,384]{3,2,1,0:T(4,128)(2,1)} reshape(bf16[1728,1536]{1,0:T(8,128)(2,1)} %convolution_convert_fusion) | data formatting | bytes 10616832 | tf_op jit(solution)/shard_map/reshape | solution.py:95
  394.6 5.5 %copy.17 = bf16[4,432,4,384]{3,1,2,0:T(8,128)(2,1)} copy(bf16[4,432,4,384]{3,2,1,0:T(4,128)(2,1)} %reshape.98) | data formatting | bytes 10616832 | tf_op jit(solution)/shard_map/reshape | solution.py:95
  400.1 4.0 fusion.28
  404.2 5.1 fusion.20
  409.4 1.6 pad_maximum_fusion.1
  411.0 1.7 collective-permute-start.3
  412.7 0.6 pad_maximum_fusion.5
  413.3 4.4 fusion.9
  417.7 7.1 %fusion.3 = f32[768,1024]{1,0:T(8,128)} fusion(bf16[1728,1536]{1,0:T(8,128)(2,1)} %all-gather.4.cloned.1.call-done, bf16[1728,1536]{1,0:T(8,128)(2,1)S(1)} %bitcast.35, s32[]{:T(128)S(6)} %select_n.58), kind=kOutput, calls=%fused_computation.12 | convolution fusion | flops 2717908992 | bytes 9338884 | tf_op jit(solution)/shard_map/dot_general | solution.py:28
  424.8 75.8 %reduce-scatter.5.cloned.1.call-done = bf16[1,432,384]{2,1,0:T(8,128)(2,1)} async-done(((bf16[16,432,384]{2,1,0:T(8,128)(2,1)}), bf16[1,432,384]{2,1,0:T(8,128)(2,1)}) %reduce-scatter.5.cloned.1.call-update) | async-done | bytes 331792 | tf_op jit(solution)/shard_map/reduce_scatter | solution.py:96
  500.6 3.8 collective-permute-start.2
  504.4 3.4 maximum_add_fusion
  508.1 1.3 slice.80
  509.3 3.7 reshape.100
  513.1 3.9 collective-permute-done.2
  517.0 3.1 convolution_convert_fusion.3
  (53 shorter events, 2.6 us)
Async XLA Ops:
  7.2 184.2 %copy-start = (bf16[8,6144]{1,0:T(8,128)(2,1)S(1)}, bf16[8,6144]{1,0:T(8,128)(2,1)}, u32[]{:S(2)}) copy-start(bf16[8,6144]{1,0:T(8,128)(2,1)} %param.9) | copy-start | bytes 294916
  7.2 132.3 %all-gather.6.cloned.1.call-start = ((), (), s32[]{:S(2)}) async-start(), calls=%async_computation.5 | async-start | bytes 11280384 | tf_op jit(solution)/shard_map/all_gather | solution.py:51
  8.7 28.6 %copy-start.7 = (bf16[768,2,512]{2,1,0:T(2,128)(2,1)S(1)}, bf16[768,2,512]{2,1,0:T(2,128)(2,1)}, u32[]{:S(2)}) copy-start(bf16[768,2,512]{2,1,0:T(2,128)(2,1)} %param.10) | copy-start | bytes 4718596
  11.8 24.6 %collective-permute-start = (bf16[432,768]{1,0:T(8,128)(2,1)S(1)}, bf16[432,768]{1,0:T(8,128)(2,1)S(1)}, u32[]{:S(2)}, u32[]{:S(2)}) collective-permute-start(bf16[432,768]{1,0:T(8,128)(2,1)S(1)} %fusion.33), channel_id=1, source_target_pairs={{0,0},{1,1},{2,2},{3,3},{4,32},{5,33},{6,34},{7,35},{8,64},{9,65},... | collective-permute-start | bytes 1990664 | tf_op jit(solution)/shard_map/ppermute | solution.py:50
  36.3 0.8 copy-start.10
  37.2 208.9 %reduce-scatter.3.cloned.1.call-start = ((), (), s32[]{:S(2)}) async-start(), calls=%async_computation.2 | async-start | bytes 6635520 | tf_op jit(solution)/shard_map/reduce_scatter | solution.py:76
  37.3 1.1 copy-start.9
  38.5 78.8 %collective-permute-start.1 = (bf16[768,1536]{1,0:T(8,128)(2,1)S(1)}, bf16[768,1536]{1,0:T(8,128)(2,1)}, u32[]{:S(2)}, u32[]{:S(2)}) collective-permute-start(bf16[768,1536]{1,0:T(8,128)(2,1)S(1)} %constant_dynamic-update-slice_fusion), channel_id=1, source_target_pairs={{0,16},{16,0},{1,17},{17,1},{2,18},{18,2},{3,19},{19,3},{4,20},{20... | collective-permute-start | bytes 7077896 | tf_op jit(solution)/shard_map/ppermute | solution.py:48
  173.5 2.7 copy-start.2
  173.5 3.4 copy-start.4
  173.5 5.8 %copy-start.6 = (bf16[768,1536]{1,0:T(8,128)(2,1)S(1)}, bf16[768,1536]{1,0:T(8,128)(2,1)}, u32[]{:S(2)}) copy-start(bf16[768,1536]{1,0:T(8,128)(2,1)} %get-tuple-element.11) | copy-start | bytes 7077892
  174.5 10.9 %copy-start.3 = (bf16[216,8,4,384]{3,1,2,0:T(8,128)(2,1)}, bf16[216,8,4,384]{3,1,2,0:T(8,128)(2,1)S(1)}, u32[]{:S(2)}) copy-start(bf16[216,8,4,384]{3,1,2,0:T(8,128)(2,1)S(1)} %copy.24) | copy-start | bytes 15925252
  191.3 1.3 copy-start.8
  191.3 183.8 %all-gather.4.cloned.1.call-start = ((), (), s32[]{:S(2)}) async-start(), calls=%async_computation.3 | async-start | bytes 6635520 | tf_op jit(solution)/shard_map/all_gather | solution.py:91
  320.9 54.3 %copy-start.5 = (bf16[768,1536]{1,0:T(8,128)(2,1)S(1)}, bf16[768,1536]{1,0:T(8,128)(2,1)}, u32[]{:S(2)}) copy-start(bf16[768,1536]{1,0:T(8,128)(2,1)} %get-tuple-element.10) | copy-start | bytes 7077892
  322.1 178.5 %reduce-scatter.5.cloned.1.call-start = ((), (), s32[]{:S(2)}) async-start(), calls=%async_computation.4 | async-start | bytes 5640192 | tf_op jit(solution)/shard_map/reduce_scatter | solution.py:96
  400.1 4.1 slice-start
  400.1 4.1 slice-start.1
  409.3 3.3 copy-start.11
  409.4 8.4 %slice-start.2 = ((s8[5308416]{0:T(1024)(128)(4,1)}), s8[1114112]{0:T(1024)(128)(4,1)S(1)}, s32[]{:S(2)}) async-start(s8[5308416]{0:T(1024)(128)(4,1)} %bitcast.33), calls=%async_computation.8 | async-start | bytes 2228224
  411.0 93.4 %collective-permute-start.3 = (bf16[768,1536]{1,0:T(8,128)(2,1)}, bf16[768,1536]{1,0:T(8,128)(2,1)}, u32[]{:S(2)}, u32[]{:S(2)}) collective-permute-start(bf16[768,1536]{1,0:T(8,128)(2,1)} %pad_maximum_fusion.1), channel_id=1, source_target_pairs={{0,16},{16,0},{1,17},{17,1},{2,18},{18,2},{3,19},{19,3},{4,20},{20... | collective-permute-start | bytes 7077896 | tf_op jit(solution)/shard_map/ppermute | solution.py:108
  413.3 4.4 slice-start.3
  500.6 16.4 %collective-permute-start.2 = (bf16[432,384]{1,0:T(8,128)(2,1)}, bf16[432,384]{1,0:T(8,128)(2,1)}, u32[]{:S(2)}, u32[]{:S(2)}) collective-permute-start(bf16[432,384]{1,0:T(8,128)(2,1)} %bitcast.41), channel_id=1, source_target_pairs={{0,0},{1,1},{2,2},{3,3},{4,32},{5,33},{6,34},{7,35},{8,64},{9,65},... | collective-permute-start | bytes 995336 | tf_op jit(solution)/shard_map/ppermute | solution.py:110
  509.3 10.7 %copy-start.1 = (bf16[8,6144]{1,0:T(8,128)(2,1)S(1)}, bf16[8,6144]{1,0:T(8,128)(2,1)}, u32[]{:S(2)}) copy-start(bf16[8,6144]{1,0:T(8,128)(2,1)} %param.9) | copy-start | bytes 294916
Sparse Core Ops, SparseCore 0:
  37.3 102.1 all-gather.5
  191.5 54.6 reduce-scatter.2
  322.2 52.9 all-gather.3
  400.2 100.3 reduce-scatter.4
where the time goes:
time: 528 us; the launch traced here: 527 us
  waiting for transfers between devices  297 us (56%)
  blocking collectives  71.2 us (13%)
  local copies, waits for them, and re-layouts  63.7 us (12%)
  matrix products  46.2 us (9%)
  other arithmetic  19.1 us (4%)
  starting transfers between devices  15.7 us (3%)
  between operations  14.1 us (3%)
    ppermute x1, waiting for transfers between devices, local(): other_weights = lax.ppermute(weights, 'zl', [(0, 1), (1, 0)])  76.6 us
    reduce_scatter x1, waiting for transfers between devices, local(): back = lax.psum_scatter(back, 'hid', scatter_dimension=0, tiled=False)  75.8 us
    all_gather x1, waiting for transfers between devices, local(): mids = lax.all_gather(mids, 'y', axis=0, tiled=True)  53 us
    reduce_scatter x1, waiting for transfers between devices, local(): lax.psum_scatter(pre, 'y', scatter_dimension=0, tiled=True)  52.6 us
    dot_general x10, matrix products, dot_f32(): lax.dot_general(left, right, ((dims[0], dims[1]), ((), ())), preferred_el...  46.2 us
    psum x1, blocking collectives, local(): scores = lax.psum(score_part, 'hid')  37.8 us
    psum x1, blocking collectives, local(): margin = lax.psum(margin_part, 'hid')  33.4 us
    reshape x2, local copies, waits for them, and re-layouts, local(): parts = gathered.reshape(4, 4, CAP, 2, cols).transpose(3, 0, 2, 1, 4)  29.2 us
  transfers between devices with their start and end apart: 8, of which 7 were waited for; matrix products, arithmetic and copies ran while one was open for 7% of the time, Pallas kernels for 0%

commit v1 on v0

--- a/solution.py
+++ b/solution.py
@@ -55,7 +55,7 @@
     labels = jnp.arange(logits.shape[1], dtype=jnp.int32)
     other_logit = jnp.sum(jnp.where(other[:, None] == labels[None, :], logits, 0.0), axis=1)
     margin_part = jnp.sum(jnp.where(placed, (logits[:, 0] - other_logit)[None, :], 0.0), axis=1)
-    margin = lax.psum(margin_part, "hid")
+    margin = jnp.sum(lax.all_gather(margin_part, "hid"), axis=0)
     filled = jnp.any(placed, axis=1)
     slot_gate = jnp.where(filled, jax.nn.sigmoid(margin), 0.0)
     parts = gathered.reshape(4, 4, CAP, 2, cols).transpose(3, 0, 2, 1, 4)

time: 528 us -> 560 us (1.061)
  blocking collectives: 71.2 us -> 103 us
    unnamed x0 -> x1, blocking collectives: none -> 65.2 us
    psum x1 -> x0, blocking collectives: 33.4 us -> none  [local(): margin = lax.psum(margin_part, 'hid')]
where the time goes in v1:
time: 560 us; the launch traced here: 559 us
  waiting for transfers between devices  295 us (53%)
  blocking collectives  103 us (18%)
  local copies, waits for them, and re-layouts  64.6 us (12%)
  matrix products  46.2 us (8%)
  other arithmetic  19.1 us (3%)
  starting transfers between devices  15.7 us (3%)
  between operations  14.8 us (3%)
    ppermute x1, waiting for transfers between devices, local(): other_weights = lax.ppermute(weights, 'zl', [(0, 1), (1, 0)])  76.6 us
    reduce_scatter x1, waiting for transfers between devices, local(): back = lax.psum_scatter(back, 'hid', scatter_dimension=0, tiled=False)  75.7 us
    unnamed x1, blocking collectives  65.2 us
    all_gather x1, waiting for transfers between devices, local(): mids = lax.all_gather(mids, 'y', axis=0, tiled=True)  53.1 us
    reduce_scatter x1, waiting for transfers between devices, local(): lax.psum_scatter(pre, 'y', scatter_dimension=0, tiled=True)  51.4 us
    dot_general x10, matrix products, dot_f32(): lax.dot_general(left, right, ((dims[0], dims[1]), ((), ())), preferred_el...  46.2 us
    psum x1, blocking collectives, local(): scores = lax.psum(score_part, 'hid')  37.8 us
    reshape x2, local copies, waits for them, and re-layouts, local(): parts = gathered.reshape(4, 4, CAP, 2, cols).transpose(3, 0, 2, 1, 4)  29.2 us
  transfers between devices with their start and end apart: 8, of which 7 were waited for; matrix products, arithmetic and copies ran while one was open for 7% of the time, Pallas kernels for 0%

profile of v1, /device:TPU:24, one launch (start us, length us, event | category | flops | bytes accessed | tf_op | source)
XLA Modules:
  0.0 558.8 jit_solution(11049082813256234120)
XLA Ops:
  7.2 0.8 convert_reduce_fusion
  8.7 3.1 fusion.33
  11.8 7.9 %collective-permute-start = (bf16[432,768]{1,0:T(8,128)(2,1)S(1)}, bf16[432,768]{1,0:T(8,128)(2,1)S(1)}, u32[]{:S(2)}, u32[]{:S(2)}) collective-permute-start(bf16[432,768]{1,0:T(8,128)(2,1)S(1)} %fusion.33), channel_id=1, source_target_pairs={{0,0},{1,1},{2,2},{3,3},{4,32},{5,33},{6,34},{7,35},{8,64},{9,65},... | collective-permute-start | bytes 1990664 | tf_op jit(solution)/shard_map/ppermute | solution.py:50
  19.7 16.6 %collective-permute-done = bf16[432,768]{1,0:T(8,128)(2,1)S(1)} collective-permute-done((bf16[432,768]{1,0:T(8,128)(2,1)S(1)}, bf16[432,768]{1,0:T(8,128)(2,1)S(1)}, u32[]{:S(2)}, u32[]{:S(2)}) %collective-permute-start) | collective-permute-done | bytes 663584 | tf_op jit(solution)/shard_map/ppermute | solution.py:50
  36.3 0.8 copy-done.10
  37.8 0.6 copy-done.9
  38.5 2.2 collective-permute-start.1
  40.6 76.6 %collective-permute-done.1 = bf16[768,1536]{1,0:T(8,128)(2,1)} collective-permute-done((bf16[768,1536]{1,0:T(8,128)(2,1)S(1)}, bf16[768,1536]{1,0:T(8,128)(2,1)}, u32[]{:S(2)}, u32[]{:S(2)}) %collective-permute-start.1) | collective-permute-done | bytes 2359328 | tf_op jit(solution)/shard_map/ppermute | solution.py:48
  117.3 4.2 broadcast_select_fusion.1
  121.5 18.0 %all-gather.7.cloned.1.call-done = bf16[6912,768]{1,0:T(8,128)(2,1)} async-done(((bf16[432,768]{1,0:T(8,128)(2,1)}), bf16[6912,768]{1,0:T(8,128)(2,1)}) %all-gather.7.cloned.1.call-update) | async-done | bytes 10616848 | tf_op jit(solution)/shard_map/all_gather | solution.py:51
  139.5 20.7 %reshape.104 = bf16[4,4,432,2,384]{4,3,2,1,0:T(2,128)(2,1)} reshape(bf16[6912,768]{1,0:T(8,128)(2,1)} %all-gather.7.cloned.1.call-done) | data formatting | bytes 21233664 | tf_op jit(solution)/shard_map/reshape | solution.py:61
  160.1 8.5 %copy.26 = bf16[4,4,432,2,384]{4,1,2,0,3:T(4,128)(2,1)S(1)} copy(bf16[4,4,432,2,384]{4,3,2,1,0:T(2,128)(2,1)} %reshape.104) | data formatting | bytes 21233664 | tf_op jit(solution)/shard_map/reshape | solution.py:61
  168.7 3.8 fusion.53
  172.5 1.0 copy.22
  173.5 1.0 copy.24
  174.5 1.7 copy-done.2
  176.2 0.7 copy-done.4
  176.9 2.4 copy-done.6
  179.3 6.1 %convolution_convert_fusion.1 = bf16[1728,1024]{1,0:T(8,128)(2,1)S(1)} fusion(bf16[1728,1536]{1,0:T(8,128)(2,1)S(1)} %bitcast.30, bf16[768,1536]{1,0:T(8,128)(2,1)S(1)} %copy-done.4, bf16[768,1536]{1,0:T(8,128)(2,1)S(1)} %copy-done.6), kind=kOutput, calls=%fused_computation.6 | convolution fusion | flops 5443878912 | bytes 13565952 | tf_op jit(solution)/shard_map/dot_general | solution.py:28
  185.4 3.1 convolution_convert_fusion.2
  188.5 2.8 pad_maximum_fusion
  191.4 1.2 copy-done.8
  193.1 0.6 dynamic-slice
  194.7 51.4 %reduce-scatter.3.cloned.1.call-done = bf16[432,1536]{1,0:T(8,128)(2,1)} async-done(((bf16[1728,1536]{1,0:T(8,128)(2,1)}), bf16[432,1536]{1,0:T(8,128)(2,1)}) %reduce-scatter.3.cloned.1.call-update) | async-done | bytes 1327120 | tf_op jit(solution)/shard_map/reduce_scatter | solution.py:76
  246.1 1.6 convert_element_type.51
  248.1 37.8 %psum.7 = f32[432]{0:T(512)S(1)} all-reduce(f32[432]{0:T(512)S(1)} %multiply_reduce_fusion), channel_id=1, replica_groups=mesh['y'=4,'zl'=2,'hid'=16] {'hid'}, use_global_device_ids=true, to_apply=%region_9.10 | all-reduce | flops 432 | bytes 3456 | tf_op jit(solution)/shard_map/psum | solution.py:93
  285.9 1.0 select_reduce_fusion
  287.2 65.2 %all-reduce = f32[6912]{0:T(1024)S(1)} all-reduce(f32[6912]{0:T(1024)S(1)} %dynamic-update-slice), channel_id=2, replica_groups=mesh['y'=4,'zl'=2,'hid'=16] {'hid'}, use_global_device_ids=true, to_apply=%add | all-reduce | flops 6912 | bytes 55296
  352.5 0.6 multiply_convert_fusion.2
  353.1 1.1 pad_maximum_fusion.4
  354.3 53.1 %all-gather.5.cloned.1.call-done = bf16[1728,1536]{1,0:T(8,128)(2,1)} async-done(((bf16[432,1536]{1,0:T(8,128)(2,1)}), bf16[1728,1536]{1,0:T(8,128)(2,1)}) %all-gather.5.cloned.1.call-update) | async-done | bytes 5308432 | tf_op jit(solution)/shard_map/all_gather | solution.py:91
  407.4 9.7 %convolution_convert_fusion = bf16[1728,1536]{1,0:T(8,128)(2,1)} fusion(bf16[1728,1536]{1,0:T(8,128)(2,1)} %all-gather.5.cloned.1.call-done, bf16[768,1536]{1,0:T(8,128)(2,1)S(1)} %copy-done.5, bf16[768,1536]{1,0:T(8,128)(2,1)} %get-tuple-element.11), kind=kOutput, calls=%fused_computation.1 | convolution fusion | flops 5444763648 | bytes 13565952 | tf_op jit(solution)/shard_map/dot_general | solution.py:28
  417.1 9.7 %reshape.106 = bf16[4,432,4,384]{3,2,1,0:T(4,128)(2,1)} reshape(bf16[1728,1536]{1,0:T(8,128)(2,1)} %convolution_convert_fusion) | data formatting | bytes 10616832 | tf_op jit(solution)/shard_map/reshape | solution.py:95
  426.9 5.5 copy.17
  432.4 4.0 fusion.28
  436.4 5.1 fusion.20
  441.6 1.6 pad_maximum_fusion.1
  443.2 1.7 collective-permute-start.3
  444.9 0.6 pad_maximum_fusion.5
  445.5 4.4 fusion.9
  450.0 7.1 %fusion.3 = f32[768,1024]{1,0:T(8,128)} fusion(bf16[1728,1536]{1,0:T(8,128)(2,1)} %all-gather.5.cloned.1.call-done, bf16[1728,1536]{1,0:T(8,128)(2,1)S(1)} %bitcast.36, s32[]{:T(128)S(6)} %select_n.62), kind=kOutput, calls=%fused_computation.12 | convolution fusion | flops 2717908992 | bytes 9338884 | tf_op jit(solution)/shard_map/dot_general | solution.py:28
  457.0 75.7 %reduce-scatter.5.cloned.1.call-done = bf16[1,432,384]{2,1,0:T(8,128)(2,1)} async-done(((bf16[16,432,384]{2,1,0:T(8,128)(2,1)}), bf16[1,432,384]{2,1,0:T(8,128)(2,1)}) %reduce-scatter.5.cloned.1.call-update) | async-done | bytes 331792 | tf_op jit(solution)/shard_map/reduce_scatter | solution.py:96
  532.7 3.8 collective-permute-start.2
  536.5 3.4 maximum_add_fusion
  540.3 1.3 slice.80
  541.5 3.7 reshape.108
  545.2 3.9 collective-permute-done.2
  549.2 3.1 convolution_convert_fusion.3
  (60 shorter events, 3.4 us)
Async XLA Ops:
  7.2 184.2 %copy-start = (bf16[8,6144]{1,0:T(8,128)(2,1)S(1)}, bf16[8,6144]{1,0:T(8,128)(2,1)}, u32[]{:S(2)}) copy-start(bf16[8,6144]{1,0:T(8,128)(2,1)} %param.9) | copy-start | bytes 294916
  7.2 132.3 %all-gather.7.cloned.1.call-start = ((), (), s32[]{:S(2)}) async-start(), calls=%async_computation.5 | async-start | bytes 11280384 | tf_op jit(solution)/shard_map/all_gather | solution.py:51
  8.7 28.6 %copy-start.7 = (bf16[768,2,512]{2,1,0:T(2,128)(2,1)S(1)}, bf16[768,2,512]{2,1,0:T(2,128)(2,1)}, u32[]{:S(2)}) copy-start(bf16[768,2,512]{2,1,0:T(2,128)(2,1)} %param.10) | copy-start | bytes 4718596
  11.8 24.6 %collective-permute-start = (bf16[432,768]{1,0:T(8,128)(2,1)S(1)}, bf16[432,768]{1,0:T(8,128)(2,1)S(1)}, u32[]{:S(2)}, u32[]{:S(2)}) collective-permute-start(bf16[432,768]{1,0:T(8,128)(2,1)S(1)} %fusion.33), channel_id=1, source_target_pairs={{0,0},{1,1},{2,2},{3,3},{4,32},{5,33},{6,34},{7,35},{8,64},{9,65},... | collective-permute-start | bytes 1990664 | tf_op jit(solution)/shard_map/ppermute | solution.py:50
  36.3 0.8 copy-start.10
  37.2 208.9 %reduce-scatter.3.cloned.1.call-start = ((), (), s32[]{:S(2)}) async-start(), calls=%async_computation.2 | async-start | bytes 6635520 | tf_op jit(solution)/shard_map/reduce_scatter | solution.py:76
  37.3 1.1 copy-start.9
  38.5 78.8 %collective-permute-start.1 = (bf16[768,1536]{1,0:T(8,128)(2,1)S(1)}, bf16[768,1536]{1,0:T(8,128)(2,1)}, u32[]{:S(2)}, u32[]{:S(2)}) collective-permute-start(bf16[768,1536]{1,0:T(8,128)(2,1)S(1)} %constant_dynamic-update-slice_fusion), channel_id=1, source_target_pairs={{0,16},{16,0},{1,17},{17,1},{2,18},{18,2},{3,19},{19,3},{4,20},{20... | collective-permute-start | bytes 7077896 | tf_op jit(solution)/shard_map/ppermute | solution.py:48
  173.5 2.7 copy-start.2
  173.5 3.4 copy-start.4
  173.5 5.8 %copy-start.6 = (bf16[768,1536]{1,0:T(8,128)(2,1)S(1)}, bf16[768,1536]{1,0:T(8,128)(2,1)}, u32[]{:S(2)}) copy-start(bf16[768,1536]{1,0:T(8,128)(2,1)} %get-tuple-element.11) | copy-start | bytes 7077892
  174.5 10.9 %copy-start.3 = (bf16[216,8,4,384]{3,1,2,0:T(8,128)(2,1)}, bf16[216,8,4,384]{3,1,2,0:T(8,128)(2,1)S(1)}, u32[]{:S(2)}) copy-start(bf16[216,8,4,384]{3,1,2,0:T(8,128)(2,1)S(1)} %copy.24) | copy-start | bytes 15925252
  191.3 1.3 copy-start.8
  191.3 1.7 copy-start.12
  191.3 216.0 %all-gather.5.cloned.1.call-start = ((), (), s32[]{:S(2)}) async-start(), calls=%async_computation.3 | async-start | bytes 6635520 | tf_op jit(solution)/shard_map/all_gather | solution.py:91
  353.1 54.3 %copy-start.5 = (bf16[768,1536]{1,0:T(8,128)(2,1)S(1)}, bf16[768,1536]{1,0:T(8,128)(2,1)}, u32[]{:S(2)}) copy-start(bf16[768,1536]{1,0:T(8,128)(2,1)} %get-tuple-element.10) | copy-start | bytes 7077892
  354.2 178.5 %reduce-scatter.5.cloned.1.call-start = ((), (), s32[]{:S(2)}) async-start(), calls=%async_computation.4 | async-start | bytes 5640192 | tf_op jit(solution)/shard_map/reduce_scatter | solution.py:96
  432.3 4.1 slice-start
  432.3 4.1 slice-start.1
  441.6 3.3 copy-start.11
  441.6 8.4 %slice-start.2 = ((s8[5308416]{0:T(1024)(128)(4,1)}), s8[1114112]{0:T(1024)(128)(4,1)S(1)}, s32[]{:S(2)}) async-start(s8[5308416]{0:T(1024)(128)(4,1)} %bitcast.34), calls=%async_computation.8 | async-start | bytes 2228224
  443.2 93.3 %collective-permute-start.3 = (bf16[768,1536]{1,0:T(8,128)(2,1)}, bf16[768,1536]{1,0:T(8,128)(2,1)}, u32[]{:S(2)}, u32[]{:S(2)}) collective-permute-start(bf16[768,1536]{1,0:T(8,128)(2,1)} %pad_maximum_fusion.1), channel_id=1, source_target_pairs={{0,16},{16,0},{1,17},{17,1},{2,18},{18,2},{3,19},{19,3},{4,20},{20... | collective-permute-start | bytes 7077896 | tf_op jit(solution)/shard_map/ppermute | solution.py:108
  445.5 4.4 slice-start.3
  532.7 16.4 %collective-permute-start.2 = (bf16[432,384]{1,0:T(8,128)(2,1)}, bf16[432,384]{1,0:T(8,128)(2,1)}, u32[]{:S(2)}, u32[]{:S(2)}) collective-permute-start(bf16[432,384]{1,0:T(8,128)(2,1)} %bitcast.42), channel_id=1, source_target_pairs={{0,0},{1,1},{2,2},{3,3},{4,32},{5,33},{6,34},{7,35},{8,64},{9,65},... | collective-permute-start | bytes 995336 | tf_op jit(solution)/shard_map/ppermute | solution.py:110
  541.5 10.7 %copy-start.1 = (bf16[8,6144]{1,0:T(8,128)(2,1)S(1)}, bf16[8,6144]{1,0:T(8,128)(2,1)}, u32[]{:S(2)}) copy-start(bf16[8,6144]{1,0:T(8,128)(2,1)} %param.9) | copy-start | bytes 294916
Sparse Core Ops, SparseCore 0:
  37.3 102.1 all-gather.6
  191.5 54.6 reduce-scatter.2
  354.4 52.9 all-gather.4
  432.5 100.2 reduce-scatter.4
